TPU v7x, 32 devices: a whole 2x2x4 slice. The times are simulated.
32 devices in a mesh: fsdp: 4 (over z), tp: 8 (over y, x, core).
Axes of the slice: x: 2, y: 2, z: 4, core: 2. Of those that a mesh axis runs over, the one named last changes fastest.
Arguments:
- tokens: bfloat16 [3008, 4096], P('fsdp', 'tp'), may hold values from -6 to 6
- norm_gain: float32 [4096], replicated, may hold values from 0.5 to 1.5
- base_gate: bfloat16 [4096, 12288], P(None, 'tp'), may hold values from -0.09375 to 0.09375
- base_up: bfloat16 [4096, 12288], P(None, 'tp'), may hold values from -0.09375 to 0.09375
- base_down: bfloat16 [12288, 4096], P('tp'), may hold values from -0.0546875 to 0.0546875
- code_gate: bfloat16 [4096, 12288], P(('fsdp', 'tp')), may hold values from -4 to 4
- code_up: bfloat16 [4096, 12288], P(('fsdp', 'tp')), may hold values from -4 to 4
- scale_gate: float32 [4096, 96], P(('fsdp', 'tp')), may hold values from 0.005 to 0.05
- scale_up: float32 [4096, 96], P(('fsdp', 'tp')), may hold values from 0.005 to 0.05
- code_down: bfloat16 [12288, 4096], P(None, ('fsdp', 'tp')), may hold values from -4 to 4
- scale_down: float32 [96, 4096], P(None, ('fsdp', 'tp')), may hold values from 0.005 to 0.05
- cu_seqlens: int32 [4, 9], P('fsdp'), may hold values from 0 to 752, as said below
Outputs:
- mixed: bfloat16 [3008, 4096], P('fsdp', 'tp')
- seq_means: float32 [32, 4096], P('fsdp', 'tp')
Inputs may be any that keep to these rules, and one draw needn't show every extreme that they name: `cu_seqlens`: each row starts at 0 and rises strictly; its last entry is the group's live tokens, which fill the first slots of its 752. Over all groups the live tokens add up to exactly 1536, and some group has exactly 752.
All inputs are finite; a program needn't handle non-finite values.
Results may differ from a plain program's by a relative error of at most 0.023.
Values may be sent and summed in bfloat16 or wider, within the bound.
A program may use at most 256 MiB of HBM per device.

v0:
```python
import jax
import jax.numpy as jnp
from jax import lax
from jax.sharding import PartitionSpec as P

SEQS = 8
EPSILON = 1e-06


def dequant_rows(base_part, code_part, scales):
    height, breadth = code_part.shape
    blocks = scales.shape[1]
    spread_out = (
        code_part.astype(jnp.float32).reshape(height, blocks, breadth // blocks)
        * scales[:, :, None]
    )
    return (base_part.astype(jnp.float32) + spread_out.reshape(height, breadth)).astype(
        jnp.bfloat16
    )


def dequant_cols(base_part, code_part, scales):
    height, breadth = code_part.shape
    blocks = scales.shape[0]
    spread_out = (
        code_part.astype(jnp.float32).reshape(blocks, height // blocks, breadth)
        * scales[:, None, :]
    )
    return (base_part.astype(jnp.float32) + spread_out.reshape(height, breadth)).astype(
        jnp.bfloat16
    )


def forward(
    rows_in,
    norm_gain,
    base_gate,
    base_up,
    base_down,
    code_gate,
    code_up,
    scale_gate,
    scale_up,
    code_down,
    scale_down,
):
    gathered = lax.all_gather(rows_in, "tp", axis=1, tiled=True)
    widened = gathered.astype(jnp.float32)
    inverse = lax.rsqrt(jnp.mean(widened * widened, axis=1, keepdims=True) + EPSILON)
    normed = (widened * inverse * norm_gain[None, :]).astype(jnp.bfloat16)
    sliced = (
        lax.all_to_all(code_gate, "tp", split_axis=1, concat_axis=0, tiled=True),
        lax.all_to_all(code_up, "tp", split_axis=1, concat_axis=0, tiled=True),
        lax.all_to_all(
            scale_gate.astype(jnp.bfloat16), "tp", split_axis=1, concat_axis=0, tiled=True
        ).astype(scale_gate.dtype),
        lax.all_to_all(
            scale_up.astype(jnp.bfloat16), "tp", split_axis=1, concat_axis=0, tiled=True
        ).astype(scale_up.dtype),
    )
    pieces = (
        lax.all_gather(sliced[0], "fsdp", axis=0, tiled=True),
        lax.all_gather(sliced[1], "fsdp", axis=0, tiled=True),
        lax.all_gather(sliced[2].astype(jnp.bfloat16), "fsdp", axis=0, tiled=True).astype(
            jnp.float32
        ),
        lax.all_gather(sliced[3].astype(jnp.bfloat16), "fsdp", axis=0, tiled=True).astype(
            jnp.float32
        ),
    )
    gate_add = jnp.dot(
        normed, dequant_rows(base_gate, pieces[0], pieces[2]), preferred_element_type=jnp.float32
    )
    up_add = jnp.dot(
        normed, dequant_rows(base_up, pieces[1], pieces[3]), preferred_element_type=jnp.float32
    )
    hidden = (jax.nn.silu(gate_add) * up_add).astype(jnp.bfloat16)
    sliced_down = (
        lax.all_to_all(code_down, "tp", split_axis=0, concat_axis=1, tiled=True),
        lax.all_to_all(
            scale_down.astype(jnp.bfloat16), "tp", split_axis=0, concat_axis=1, tiled=True
        ).astype(scale_down.dtype),
    )
    pieces = (
        lax.all_gather(sliced_down[0], "fsdp", axis=1, tiled=True),
        lax.all_gather(sliced_down[1].astype(jnp.bfloat16), "fsdp", axis=1, tiled=True).astype(
            jnp.float32
        ),
    )
    block_out = jnp.dot(
        hidden, dequant_cols(base_down, pieces[0], pieces[1]), preferred_element_type=jnp.float32
    )
    summed = lax.psum_scatter(
        block_out.astype(jnp.bfloat16), "tp", scatter_dimension=1, tiled=True
    ).astype(jnp.float32)
    return (rows_in.astype(jnp.float32) + summed).astype(jnp.bfloat16)


def shards(
    tokens,
    norm_gain,
    base_gate,
    base_up,
    base_down,
    code_gate,
    code_up,
    scale_gate,
    scale_up,
    code_down,
    scale_down,
    cu_seqlens,
):
    capacity = tokens.shape[0]
    bounds = cu_seqlens[0]
    live_count = bounds[SEQS]
    positions = jnp.arange(capacity, dtype=jnp.int32)
    mixed_rows = forward(
        tokens,
        norm_gain,
        base_gate,
        base_up,
        base_down,
        code_gate,
        code_up,
        scale_gate,
        scale_up,
        code_down,
        scale_down,
    )
    mixed_rows = jnp.where(
        (positions < live_count)[:, None], mixed_rows, jnp.zeros((), jnp.bfloat16)
    )
    member = (positions[None, :] >= bounds[:-1, None]) & (positions[None, :] < bounds[1:, None])
    seq_sums = jnp.dot(member.astype(jnp.bfloat16), mixed_rows, preferred_element_type=jnp.float32)
    lengths = (bounds[1:] - bounds[:-1]).astype(jnp.float32)
    return (mixed_rows, seq_sums / lengths[:, None])


def solution(mesh):
    placed = (
        P("fsdp", "tp"),
        P(),
        P(None, "tp"),
        P(None, "tp"),
        P("tp", None),
        P(("fsdp", "tp"), None),
        P(("fsdp", "tp"), None),
        P(("fsdp", "tp"), None),
        P(("fsdp", "tp"), None),
        P(None, ("fsdp", "tp")),
        P(None, ("fsdp", "tp")),
        P("fsdp", None),
    )
    return jax.shard_map(
        shards,
        mesh=mesh,
        in_specs=placed,
        out_specs=(P("fsdp", "tp"), P("fsdp", "tp")),
        check_vma=False,
    )
```

profile of v0, /device:TPU:0, one launch (start us, length us, event | category | flops | bytes accessed | tf_op | source)
XLA Modules:
  0.0 834.5 jit_solution(9441921378246151597)
XLA Ops:
  7.9 3.5 copy.26
  11.4 57.3 %all_to_all.114 = bf16[128,8,1536]{0,2,1:T(8,128)(2,1)S(1)} all-to-all(bf16[128,8,1536]{0,2,1:T(8,128)(2,1)S(1)} %bitcast.81), channel_id=1, replica_groups=mesh['fsdp'=4,'tp'=8] {'tp'}, dimensions={1} | all-to-all | bytes 6291456 | tf_op jit(solution)/shard_map/all_to_all | solution.py:52
  71.0 3.5 copy.30
  74.4 40.3 %all_to_all.115 = bf16[128,8,1536]{0,2,1:T(8,128)(2,1)S(1)} all-to-all(bf16[128,8,1536]{0,2,1:T(8,128)(2,1)S(1)} %bitcast.82), channel_id=1, replica_groups=mesh['fsdp'=4,'tp'=8] {'tp'}, dimensions={1} | all-to-all | bytes 6291456 | tf_op jit(solution)/shard_map/all_to_all | solution.py:53
  116.9 41.4 %all_to_all.116 = bf16[8,1536,128]{2,1,0:T(8,128)(2,1)S(1)} all-to-all(bf16[8,1536,128]{2,1,0:T(8,128)(2,1)} %bitcast.83), channel_id=1, replica_groups=mesh['fsdp'=4,'tp'=8] {'tp'}, dimensions={0} | all-to-all | bytes 6291456 | tf_op jit(solution)/shard_map/all_to_all | solution.py:79
  161.1 3.3 all-to-all-start.1
  164.5 16.8 %copy.25 = bf16[4096,1536]{0,1:T(8,128)(2,1)} copy(bf16[4096,1536]{1,0:T(8,128)(2,1)} %param.14) | data formatting | bytes 25165824 | tf_op args[2]
  181.3 16.1 %copy.29 = bf16[4096,1536]{0,1:T(8,128)(2,1)} copy(bf16[4096,1536]{1,0:T(8,128)(2,1)} %param.15) | data formatting | bytes 25165824 | tf_op args[3]
  198.6 4.2 all-to-all-start.3
  202.9 22.0 %all_gather.23 = bf16[4096,12]{0,1:T(8,128)(2,1)S(1)} all-gather(bf16[1024,12]{0,1:T(8,128)(2,1)S(1)} %bitcast.84), channel_id=1, replica_groups=mesh['fsdp'=4,'tp'=8] {'fsdp'}, dimensions={0}, use_global_device_ids=true | all-gather | bytes 122880 | tf_op jit(solution)/shard_map/all_gather | solution.py:64
  224.9 4.0 all-to-all-start.5
  229.0 26.2 %all_gather.25 = bf16[4096,12]{0,1:T(8,128)(2,1)S(1)} all-gather(bf16[1024,12]{0,1:T(8,128)(2,1)S(1)} %bitcast.85), channel_id=1, replica_groups=mesh['fsdp'=4,'tp'=8] {'fsdp'}, dimensions={0}, use_global_device_ids=true | all-gather | bytes 122880 | tf_op jit(solution)/shard_map/all_gather | solution.py:67
  255.3 19.9 %all_gather.27 = bf16[12,4096]{1,0:T(8,128)(2,1)S(1)} all-gather(bf16[12,1024]{1,0:T(8,128)(2,1)S(1)} %bitcast.86), channel_id=1, replica_groups=mesh['fsdp'=4,'tp'=8] {'fsdp'}, dimensions={1}, use_global_device_ids=true | all-gather | bytes 122880 | tf_op jit(solution)/shard_map/all_gather | solution.py:86
  275.3 4.0 fusion.6
  279.3 28.5 %all-gather.7.cloned.1.call-done = bf16[4096,1536]{0,1:T(8,128)(2,1)} async-done(((bf16[1024,1536]{0,1:T(8,128)(2,1)}), bf16[4096,1536]{0,1:T(8,128)(2,1)}) %all-gather.7.cloned.1.call-update) | async-done | bytes 12582928 | tf_op jit(solution)/shard_map/all_gather | solution.py:62
  307.8 16.4 %fusion.5 = bf16[4096,1536]{0,1:T(8,128)(2,1)} fusion(bf16[4096,1536]{0,1:T(8,128)(2,1)} %all-gather.7.cloned.1.call-done, bf16[4096,1536]{0,1:T(8,128)(2,1)} %copy.25, f32[4096,12]{0,1:T(8,128)S(1)} %convert_element_type.86), kind=kLoop, calls=%fused_computation.8 | loop fusion | flops 31457280 | bytes 37945344 | tf_op jit(solution)/shard_map/convert_element_type | solution.py:17
  324.2 201.6 %all-gather.9.cloned.1.call-done = bf16[4096,1536]{0,1:T(8,128)(2,1)} async-done(((bf16[1024,1536]{0,1:T(8,128)(2,1)}), bf16[4096,1536]{0,1:T(8,128)(2,1)}) %all-gather.9.cloned.1.call-update) | async-done | bytes 12582928 | tf_op jit(solution)/shard_map/all_gather | solution.py:63
  525.8 16.8 %fusion.3 = bf16[4096,1536]{0,1:T(8,128)(2,1)} fusion(bf16[4096,1536]{0,1:T(8,128)(2,1)} %all-gather.9.cloned.1.call-done, bf16[4096,1536]{0,1:T(8,128)(2,1)} %copy.29, f32[4096,12]{0,1:T(8,128)S(1)} %convert_element_type.91), kind=kLoop, calls=%fused_computation.5 | loop fusion | flops 31457280 | bytes 37945344 | tf_op jit(solution)/shard_map/convert_element_type | solution.py:17
  544.3 13.5 %fusion.12 = f32[752,1536]{1,0:T(8,128)} fusion(bf16[4096,1536]{0,1:T(8,128)(2,1)S(1)} %copy-done, bf16[752,4096]{1,0:T(8,128)(2,1)} %all-gather.5.cloned.1.call-done, f32[4096]{0:T(1024)S(1)} %copy-done.7, f32[752]{0:T(1024)S(1)} %add_rsqrt_fusion), kind=kOutput, calls=%fused_computation.20 | convolution fusion | flops 9474670592 | bytes 23382976 | tf_op jit(solution)/shard_map/dot_general | solution.py:71
  557.8 16.7 %multiply_convert_fusion.clone.4 = bf16[752,1536]{1,0:T(8,128)(2,1)} fusion(f32[752,1536]{1,0:T(8,128)} %fusion.12, bf16[4096,1536]{0,1:T(8,128)(2,1)} %fusion.3, bf16[752,4096]{1,0:T(8,128)(2,1)} %all-gather.5.cloned.1.call-done, f32[4096]{0:T(1024)S(1)} %copy-done.7, f32[752]{0:T(1024)S(1)} %add_rsqrt_fusion), kind=kOutput, calls=%fused_computation.15.clone.clone.clone.1 | convolution fusion | flops 9481601024 | bytes 25693120 | tf_op jit(solution)/shard_map/dot_general | solution.py:74
  574.5 169.1 %all-gather.11.cloned.1.call-done = bf16[1536,4096]{1,0:T(8,128)(2,1)} async-done(((bf16[1536,1024]{1,0:T(8,128)(2,1)}), bf16[1536,4096]{1,0:T(8,128)(2,1)}) %all-gather.11.cloned.1.call-update) | async-done | bytes 12582928 | tf_op jit(solution)/shard_map/all_gather | solution.py:85
  743.6 11.4 %fusion.1 = bf16[1536,4096]{1,0:T(8,128)(2,1)S(1)} fusion(bf16[1536,4096]{1,0:T(8,128)(2,1)} %all-gather.11.cloned.1.call-done, bf16[1536,4096]{1,0:T(8,128)(2,1)} %param.16, f32[12,4096]{1,0:T(8,128)S(1)} %convert_element_type.97), kind=kLoop, calls=%fused_computation.2 | loop fusion | flops 31457280 | bytes 37945344 | tf_op jit(solution)/shard_map/convert_element_type | solution.py:29
  755.1 11.5 %convolution_convert_fusion = bf16[752,4096]{1,0:T(8,128)(2,1)} fusion(bf16[1536,4096]{1,0:T(8,128)(2,1)S(1)} %fusion.1, bf16[752,1536]{1,0:T(8,128)(2,1)S(1)} %copy-done.8), kind=kOutput, calls=%fused_computation.14 | convolution fusion | flops 9465430016 | bytes 21053440 | tf_op jit(solution)/shard_map/dot_general | solution.py:90
  768.0 57.7 %reduce-scatter.2.cloned.1.call-done = bf16[752,512]{1,0:T(8,128)(2,1)} async-done(((bf16[752,4096]{1,0:T(8,128)(2,1)}), bf16[752,512]{1,0:T(8,128)(2,1)}) %reduce-scatter.2.cloned.1.call-update) | async-done | bytes 770064 | tf_op jit(solution)/shard_map/reduce_scatter | solution.py:93
  (60 shorter events, 14.8 us)
Async XLA Ops:
  7.2 268.1 %all-gather.5.cloned.1.call-start = ((), (), s32[]{:S(2)}) async-start(), calls=%async_computation.7 | async-start | bytes 6930432 | tf_op jit(solution)/shard_map/all_gather | solution.py:47
  7.9 299.9 %all-gather.7.cloned.1.call-start = ((), (), s32[]{:S(2)}) async-start(), calls=%async_computation.8 | async-start | bytes 15728640 | tf_op jit(solution)/shard_map/all_gather | solution.py:62
  70.9 454.9 %all-gather.9.cloned.1.call-start = ((), (), s32[]{:S(2)}) async-start(), calls=%async_computation.9 | async-start | bytes 15728640 | tf_op jit(solution)/shard_map/all_gather | solution.py:63
  114.7 45.8 %copy-start.3 = (f32[128,96]{0,1:T(8,128)S(1)}, f32[128,96]{0,1:T(8,128)}, u32[]{:S(2)}) copy-start(f32[128,96]{0,1:T(8,128)} %param.19) | copy-start | bytes 147460
  116.9 626.8 %all-gather.11.cloned.1.call-start = ((), (), s32[]{:S(2)}) async-start(), calls=%async_computation.10 | async-start | bytes 15728640 | tf_op jit(solution)/shard_map/all_gather | solution.py:85
  161.1 37.5 %all-to-all-start.1 = ((bf16[128,8,12]{0,2,1:T(8,128)(2,1)}), bf16[128,8,12]{0,2,1:T(8,128)(2,1)S(1)}, u32[]{:S(2)}, u32[]{:S(2)}) async-start(bf16[128,8,12]{0,2,1:T(8,128)(2,1)} %all_to_all.88), calls=%async_computation.1 | async-start | bytes 65536 | tf_op jit(solution)/shard_map/all_to_all | solution.py:54
  181.3 16.1 %copy-start.4 = (f32[128,96]{0,1:T(8,128)S(1)}, f32[128,96]{0,1:T(8,128)}, u32[]{:S(2)}) copy-start(f32[128,96]{0,1:T(8,128)} %param.20) | copy-start | bytes 147460
  181.3 16.7 %copy-start.5 = (f32[96,128]{1,0:T(8,128)S(1)}, f32[96,128]{1,0:T(8,128)}, u32[]{:S(2)}) copy-start(f32[96,128]{1,0:T(8,128)} %param.22) | copy-start | bytes 147460
  198.6 26.2 %all-to-all-start.3 = ((bf16[128,8,12]{0,2,1:T(8,128)(2,1)}), bf16[128,8,12]{0,2,1:T(8,128)(2,1)S(1)}, u32[]{:S(2)}, u32[]{:S(2)}) async-start(bf16[128,8,12]{0,2,1:T(8,128)(2,1)} %all_to_all.96), calls=%async_computation.3 | async-start | bytes 65536 | tf_op jit(solution)/shard_map/all_to_all | solution.py:57
  224.9 30.4 %all-to-all-start.5 = ((bf16[8,12,128]{2,1,0:T(8,128)(2,1)}), bf16[8,12,128]{2,1,0:T(8,128)(2,1)S(1)}, u32[]{:S(2)}, u32[]{:S(2)}) async-start(bf16[8,12,128]{2,1,0:T(8,128)(2,1)} %all_to_all.104), calls=%async_computation.5 | async-start | bytes 65536 | tf_op jit(solution)/shard_map/all_to_all | solution.py:80
  228.9 596.8 %reduce-scatter.2.cloned.1.call-start = ((), (), s32[]{:S(2)}) async-start(), calls=%async_computation.11 | async-start | bytes 6930432 | tf_op jit(solution)/shard_map/reduce_scatter | solution.py:93
  324.2 218.4 %copy-start.7 = (f32[4096]{0:T(1024)S(1)}, f32[4096]{0:T(1024)}, u32[]{:S(2)}) copy-start(f32[4096]{0:T(1024)} %param.13) | copy-start | bytes 49156
  525.8 18.5 %copy-start = (bf16[4096,1536]{0,1:T(8,128)(2,1)S(1)}, bf16[4096,1536]{0,1:T(8,128)(2,1)}, u32[]{:S(2)}) copy-start(bf16[4096,1536]{0,1:T(8,128)(2,1)} %fusion.5) | copy-start | bytes 37748740
  743.6 11.4 %copy-start.8 = (bf16[752,1536]{1,0:T(8,128)(2,1)S(1)}, bf16[752,1536]{1,0:T(8,128)(2,1)}, u32[]{:S(2)}) copy-start(bf16[752,1536]{1,0:T(8,128)(2,1)} %multiply_convert_fusion.clone.4) | copy-start | bytes 6930436
  755.0 11.6 %copy-start.6 = (s32[1,9]{1,0:T(1,128)S(1)}, s32[1,9]{1,0:T(1,128)}, u32[]{:S(2)}) copy-start(s32[1,9]{1,0:T(1,128)} %param.23) | copy-start | bytes 112
  755.1 70.7 %copy-start.1 = (bf16[752,512]{1,0:T(8,128)(2,1)S(1)}, bf16[752,512]{1,0:T(8,128)(2,1)}, u32[]{:S(2)}) copy-start(bf16[752,512]{1,0:T(8,128)(2,1)} %param.12) | copy-start | bytes 2310148
  827.1 0.9 copy-start.2
Sparse Core Ops, SparseCore 0:
  9.8 71.2 all-gather.4
  82.7 225.0 all-gather.6
  309.4 216.4 all-gather.8
  527.2 216.3 all-gather.10
  766.7 58.9 reduce-scatter.1
where the time goes:
time: 836 us; the launch traced here: 835 us
  waiting for transfers between devices  458 us (55%)
  blocking collectives  207 us (25%)
  other arithmetic  50.8 us (6%)
  local copies, waits for them, and re-layouts  50.6 us (6%)
  matrix products  42.6 us (5%)
  between operations  14 us (2%)
  starting transfers between devices  11.7 us (1%)
    all_gather x1, waiting for transfers between devices, forward(): lax.all_gather(sliced[1], 'fsdp', axis=0, tiled=True)  202 us
    all_gather x1, waiting for transfers between devices, forward(): lax.all_gather(sliced_down[0], 'fsdp', axis=1, tiled=True)  169 us
    reduce_scatter x1, waiting for transfers between devices, forward(): lax.psum_scatter(block_out.astype(jnp.bfloat16), 'tp', scatter_dimension=...  57.7 us
    all_to_all x1, blocking collectives, forward(): lax.all_to_all(code_gate, 'tp', split_axis=1, concat_axis=0, tiled=True)  57.3 us
    unnamed x28, local copies, waits for them, and re-layouts  41.6 us
    all_to_all x1, blocking collectives, forward(): lax.all_to_all(code_down, 'tp', split_axis=0, concat_axis=1, tiled=True)  41.4 us
    all_to_all x1, blocking collectives, forward(): lax.all_to_all(code_up, 'tp', split_axis=1, concat_axis=0, tiled=True)  40.3 us
    convert_element_type x2, other arithmetic, dequant_rows(): (base_part.astype(jnp.float32) + spread_out.reshape(height, breadth)).ast...  33.3 us
  transfers between devices with their start and end apart: 8, of which 4 were waited for; matrix products, arithmetic and copies ran while one was open for 14% of the time, Pallas kernels for 0%

commit v1 on v0

--- a/solution.py
+++ b/solution.py
@@ -49,7 +49,12 @@
     inverse = lax.rsqrt(jnp.mean(widened * widened, axis=1, keepdims=True) + EPSILON)
     normed = (widened * inverse * norm_gain[None, :]).astype(jnp.bfloat16)
     sliced = (
-        lax.all_to_all(code_gate, "tp", split_axis=1, concat_axis=0, tiled=True),
+        jnp.concatenate(
+            lax.all_to_all(
+                jnp.stack(jnp.split(code_gate, lax.axis_size("tp"), axis=1)), "tp", 0, 0
+            ),
+            axis=0,
+        ),
         lax.all_to_all(code_up, "tp", split_axis=1, concat_axis=0, tiled=True),
         lax.all_to_all(
             scale_gate.astype(jnp.bfloat16), "tp", split_axis=1, concat_axis=0, tiled=True

time: 836 us -> 839 us (level)
    unnamed x28 -> x36, local copies, waits for them, and re-layouts: 41.6 us -> 46.6 us
where the time goes in v1:
time: 839 us; the launch traced here: 837 us
  waiting for transfers between devices  456 us (54%)
  blocking collectives  205 us (24%)
  local copies, waits for them, and re-layouts  57.4 us (7%)
  other arithmetic  51 us (6%)
  matrix products  42.6 us (5%)
  between operations  14 us (2%)
  starting transfers between devices  11.5 us (1%)
    all_gather x1, waiting for transfers between devices, forward(): lax.all_gather(sliced[1], 'fsdp', axis=0, tiled=True)  201 us
    all_gather x1, waiting for transfers between devices, forward(): lax.all_gather(sliced_down[0], 'fsdp', axis=1, tiled=True)  169 us
    all_to_all x1, blocking collectives, forward(): lax.all_to_all(jnp.stack(jnp.split(code_gate, lax.axis_size('tp'), axis=1...  60.6 us
    reduce_scatter x1, waiting for transfers between devices, forward(): lax.psum_scatter(block_out.astype(jnp.bfloat16), 'tp', scatter_dimension=...  57.1 us
    unnamed x36, local copies, waits for them, and re-layouts  46.6 us
    all_to_all x1, blocking collectives, forward(): lax.all_to_all(code_up, 'tp', split_axis=1, concat_axis=0, tiled=True)  40.3 us
    all_to_all x1, blocking collectives, forward(): lax.all_to_all(code_down, 'tp', split_axis=0, concat_axis=1, tiled=True)  40.3 us
    convert_element_type x2, other arithmetic, dequant_rows(): (base_part.astype(jnp.float32) + spread_out.reshape(height, breadth)).ast...  33.4 us
  transfers between devices with their start and end apart: 8, of which 4 were waited for; matrix products, arithmetic and copies ran while one was open for 14% of the time, Pallas kernels for 0%

profile of v1, /device:TPU:0, one launch (start us, length us, event | category | flops | bytes accessed | tf_op | source)
XLA Modules:
  0.0 837.4 jit_solution(13361525801028013734)
XLA Ops:
  16.2 60.6 %all_to_all.100 = bf16[8,128,1536]{2,1,0:T(8,128)(2,1)S(1)} all-to-all(bf16[8,128,1536]{2,1,0:T(8,128)(2,1)S(1)} %bitcast_dynamic-update-slice_fusion), channel_id=1, replica_groups=mesh['fsdp'=4,'tp'=8] {'tp'}, dimensions={0} | all-to-all | bytes 6291456 | tf_op jit(solution)/shard_map/all_to_all | solution.py:53
  76.7 3.0 copy.33
  79.8 3.5 copy.28
  83.3 40.3 %all_to_all.101 = bf16[128,8,1536]{0,2,1:T(8,128)(2,1)S(1)} all-to-all(bf16[128,8,1536]{0,2,1:T(8,128)(2,1)S(1)} %bitcast.92), channel_id=1, replica_groups=mesh['fsdp'=4,'tp'=8] {'tp'}, dimensions={1} | all-to-all | bytes 6291456 | tf_op jit(solution)/shard_map/all_to_all | solution.py:58
  126.6 40.3 %all_to_all.102 = bf16[8,1536,128]{2,1,0:T(8,128)(2,1)S(1)} all-to-all(bf16[8,1536,128]{2,1,0:T(8,128)(2,1)S(1)} %bitcast.93), channel_id=1, replica_groups=mesh['fsdp'=4,'tp'=8] {'tp'}, dimensions={0} | all-to-all | bytes 6291456 | tf_op jit(solution)/shard_map/all_to_all | solution.py:84
  169.6 3.3 all-to-all-start.1
  173.0 15.9 %copy.24 = bf16[4096,1536]{0,1:T(8,128)(2,1)} copy(bf16[4096,1536]{1,0:T(8,128)(2,1)} %param.14) | data formatting | bytes 25165824 | tf_op args[2]
  188.9 16.9 %copy.27 = bf16[4096,1536]{0,1:T(8,128)(2,1)} copy(bf16[4096,1536]{1,0:T(8,128)(2,1)} %param.15) | data formatting | bytes 25165824 | tf_op args[3]
  207.1 4.1 all-to-all-start.3
  211.2 16.9 %all_gather.23 = bf16[4096,12]{0,1:T(8,128)(2,1)S(1)} all-gather(bf16[1024,12]{0,1:T(8,128)(2,1)S(1)} %bitcast.94), channel_id=1, replica_groups=mesh['fsdp'=4,'tp'=8] {'fsdp'}, dimensions={0}, use_global_device_ids=true | all-gather | bytes 122880 | tf_op jit(solution)/shard_map/all_gather | solution.py:69
  228.2 3.9 all-to-all-start.5
  232.1 27.4 %all_gather.25 = bf16[4096,12]{0,1:T(8,128)(2,1)S(1)} all-gather(bf16[1024,12]{0,1:T(8,128)(2,1)S(1)} %bitcast.95), channel_id=1, replica_groups=mesh['fsdp'=4,'tp'=8] {'fsdp'}, dimensions={0}, use_global_device_ids=true | all-gather | bytes 122880 | tf_op jit(solution)/shard_map/all_gather | solution.py:72
  259.6 19.4 %all_gather.27 = bf16[12,4096]{1,0:T(8,128)(2,1)S(1)} all-gather(bf16[12,1024]{1,0:T(8,128)(2,1)S(1)} %bitcast.96), channel_id=1, replica_groups=mesh['fsdp'=4,'tp'=8] {'fsdp'}, dimensions={1}, use_global_device_ids=true | all-gather | bytes 122880 | tf_op jit(solution)/shard_map/all_gather | solution.py:91
  279.1 4.0 fusion.6
  283.2 27.6 %all-gather.7.cloned.1.call-done = bf16[4096,1536]{0,1:T(8,128)(2,1)} async-done(((bf16[1024,1536]{0,1:T(8,128)(2,1)}), bf16[4096,1536]{0,1:T(8,128)(2,1)}) %all-gather.7.cloned.1.call-update) | async-done | bytes 12582928 | tf_op jit(solution)/shard_map/all_gather | solution.py:67
  310.8 16.5 %fusion.5 = bf16[4096,1536]{0,1:T(8,128)(2,1)} fusion(bf16[4096,1536]{0,1:T(8,128)(2,1)} %all-gather.7.cloned.1.call-done, bf16[4096,1536]{0,1:T(8,128)(2,1)} %copy.24, f32[4096,12]{0,1:T(8,128)S(1)} %convert_element_type.86), kind=kLoop, calls=%fused_computation.8 | loop fusion | flops 31457280 | bytes 37945344 | tf_op jit(solution)/shard_map/convert_element_type | solution.py:17
  327.3 201.5 %all-gather.9.cloned.1.call-done = bf16[4096,1536]{0,1:T(8,128)(2,1)} async-done(((bf16[1024,1536]{0,1:T(8,128)(2,1)}), bf16[4096,1536]{0,1:T(8,128)(2,1)}) %all-gather.9.cloned.1.call-update) | async-done | bytes 12582928 | tf_op jit(solution)/shard_map/all_gather | solution.py:68
  528.8 16.9 %fusion.3 = bf16[4096,1536]{0,1:T(8,128)(2,1)} fusion(bf16[4096,1536]{0,1:T(8,128)(2,1)} %all-gather.9.cloned.1.call-done, bf16[4096,1536]{0,1:T(8,128)(2,1)} %copy.27, f32[4096,12]{0,1:T(8,128)S(1)} %convert_element_type.91), kind=kLoop, calls=%fused_computation.5 | loop fusion | flops 31457280 | bytes 37945344 | tf_op jit(solution)/shard_map/convert_element_type | solution.py:17
  547.3 13.5 %fusion.12 = f32[752,1536]{1,0:T(8,128)} fusion(bf16[4096,1536]{0,1:T(8,128)(2,1)S(1)} %copy-done, bf16[752,4096]{1,0:T(8,128)(2,1)} %all-gather.5.cloned.1.call-done, f32[4096]{0:T(1024)S(1)} %copy-done.8, f32[752]{0:T(1024)S(1)} %add_rsqrt_fusion), kind=kOutput, calls=%fused_computation.19 | convolution fusion | flops 9474670592 | bytes 23382976 | tf_op jit(solution)/shard_map/dot_general | solution.py:76
  560.8 16.7 %multiply_convert_fusion.clone.4 = bf16[752,1536]{1,0:T(8,128)(2,1)} fusion(f32[752,1536]{1,0:T(8,128)} %fusion.12, bf16[4096,1536]{0,1:T(8,128)(2,1)} %fusion.3, bf16[752,4096]{1,0:T(8,128)(2,1)} %all-gather.5.cloned.1.call-done, f32[4096]{0:T(1024)S(1)} %copy-done.8, f32[752]{0:T(1024)S(1)} %add_rsqrt_fusion), kind=kOutput, calls=%fused_computation.15.clone.clone.clone.1 | convolution fusion | flops 9481601024 | bytes 25693120 | tf_op jit(solution)/shard_map/dot_general | solution.py:79
  577.6 169.1 %all-gather.11.cloned.1.call-done = bf16[1536,4096]{1,0:T(8,128)(2,1)} async-done(((bf16[1536,1024]{1,0:T(8,128)(2,1)}), bf16[1536,4096]{1,0:T(8,128)(2,1)}) %all-gather.11.cloned.1.call-update) | async-done | bytes 12582928 | tf_op jit(solution)/shard_map/all_gather | solution.py:90
  746.6 11.4 %fusion.1 = bf16[1536,4096]{1,0:T(8,128)(2,1)S(1)} fusion(bf16[1536,4096]{1,0:T(8,128)(2,1)} %all-gather.11.cloned.1.call-done, bf16[1536,4096]{1,0:T(8,128)(2,1)} %param.16, f32[12,4096]{1,0:T(8,128)S(1)} %convert_element_type.97), kind=kLoop, calls=%fused_computation.2 | loop fusion | flops 31457280 | bytes 37945344 | tf_op jit(solution)/shard_map/convert_element_type | solution.py:29
  758.0 11.4 %convolution_convert_fusion = bf16[752,4096]{1,0:T(8,128)(2,1)} fusion(bf16[1536,4096]{1,0:T(8,128)(2,1)S(1)} %fusion.1, bf16[752,1536]{1,0:T(8,128)(2,1)S(1)} %copy-done.9), kind=kOutput, calls=%fused_computation.14 | convolution fusion | flops 9465430016 | bytes 21053440 | tf_op jit(solution)/shard_map/dot_general | solution.py:95
  771.5 57.1 %reduce-scatter.2.cloned.1.call-done = bf16[752,512]{1,0:T(8,128)(2,1)} async-done(((bf16[752,4096]{1,0:T(8,128)(2,1)}), bf16[752,512]{1,0:T(8,128)(2,1)}) %reduce-scatter.2.cloned.1.call-update) | async-done | bytes 770064 | tf_op jit(solution)/shard_map/reduce_scatter | solution.py:98
  (69 shorter events, 22.2 us)
Async XLA Ops:
  7.2 272.0 %all-gather.5.cloned.1.call-start = ((), (), s32[]{:S(2)}) async-start(), calls=%async_computation.7 | async-start | bytes 6930432 | tf_op jit(solution)/shard_map/all_gather | solution.py:47
  7.9 302.9 %all-gather.7.cloned.1.call-start = ((), (), s32[]{:S(2)}) async-start(), calls=%async_computation.8 | async-start | bytes 15728640 | tf_op jit(solution)/shard_map/all_gather | solution.py:67
  79.7 449.1 %all-gather.9.cloned.1.call-start = ((), (), s32[]{:S(2)}) async-start(), calls=%async_computation.9 | async-start | bytes 15728640 | tf_op jit(solution)/shard_map/all_gather | solution.py:68
  123.5 3.0 copy-start.1
  125.7 620.9 %all-gather.11.cloned.1.call-start = ((), (), s32[]{:S(2)}) async-start(), calls=%async_computation.10 | async-start | bytes 15728640 | tf_op jit(solution)/shard_map/all_gather | solution.py:90
  166.8 2.2 copy-start.4
  169.6 37.4 %all-to-all-start.1 = ((bf16[128,8,12]{0,2,1:T(8,128)(2,1)}), bf16[128,8,12]{0,2,1:T(8,128)(2,1)S(1)}, u32[]{:S(2)}, u32[]{:S(2)}) async-start(bf16[128,8,12]{0,2,1:T(8,128)(2,1)} %all_to_all.74), calls=%async_computation.1 | async-start | bytes 65536 | tf_op jit(solution)/shard_map/all_to_all | solution.py:59
  188.9 16.9 %copy-start.5 = (f32[128,96]{0,1:T(8,128)S(1)}, f32[128,96]{0,1:T(8,128)}, u32[]{:S(2)}) copy-start(f32[128,96]{0,1:T(8,128)} %param.20) | copy-start | bytes 147460
  188.9 17.5 %copy-start.6 = (f32[96,128]{1,0:T(8,128)S(1)}, f32[96,128]{1,0:T(8,128)}, u32[]{:S(2)}) copy-start(f32[96,128]{1,0:T(8,128)} %param.22) | copy-start | bytes 147460
  207.1 21.1 %all-to-all-start.3 = ((bf16[128,8,12]{0,2,1:T(8,128)(2,1)}), bf16[128,8,12]{0,2,1:T(8,128)(2,1)S(1)}, u32[]{:S(2)}, u32[]{:S(2)}) async-start(bf16[128,8,12]{0,2,1:T(8,128)(2,1)} %all_to_all.82), calls=%async_computation.3 | async-start | bytes 65536 | tf_op jit(solution)/shard_map/all_to_all | solution.py:62
  228.2 31.4 %all-to-all-start.5 = ((bf16[8,12,128]{2,1,0:T(8,128)(2,1)}), bf16[8,12,128]{2,1,0:T(8,128)(2,1)S(1)}, u32[]{:S(2)}, u32[]{:S(2)}) async-start(bf16[8,12,128]{2,1,0:T(8,128)(2,1)} %all_to_all.90), calls=%async_computation.5 | async-start | bytes 65536 | tf_op jit(solution)/shard_map/all_to_all | solution.py:85
  232.0 596.5 %reduce-scatter.2.cloned.1.call-start = ((), (), s32[]{:S(2)}) async-start(), calls=%async_computation.11 | async-start | bytes 6930432 | tf_op jit(solution)/shard_map/reduce_scatter | solution.py:98
  327.3 218.4 %copy-start.8 = (f32[4096]{0:T(1024)S(1)}, f32[4096]{0:T(1024)}, u32[]{:S(2)}) copy-start(f32[4096]{0:T(1024)} %param.13) | copy-start | bytes 49156
  528.8 18.5 %copy-start = (bf16[4096,1536]{0,1:T(8,128)(2,1)S(1)}, bf16[4096,1536]{0,1:T(8,128)(2,1)}, u32[]{:S(2)}) copy-start(bf16[4096,1536]{0,1:T(8,128)(2,1)} %fusion.5) | copy-start | bytes 37748740
  746.6 11.4 %copy-start.9 = (bf16[752,1536]{1,0:T(8,128)(2,1)S(1)}, bf16[752,1536]{1,0:T(8,128)(2,1)}, u32[]{:S(2)}) copy-start(bf16[752,1536]{1,0:T(8,128)(2,1)} %multiply_convert_fusion.clone.4) | copy-start | bytes 6930436
  769.4 0.7 copy-start.7
  769.4 59.1 %copy-start.2 = (bf16[752,512]{1,0:T(8,128)(2,1)S(1)}, bf16[752,512]{1,0:T(8,128)(2,1)}, u32[]{:S(2)}) copy-start(bf16[752,512]{1,0:T(8,128)(2,1)} %param.12) | copy-start | bytes 2310148
  830.0 0.9 copy-start.3
Sparse Core Ops, SparseCore 0:
  9.8 74.9 all-gather.4
  86.4 224.3 all-gather.6
  312.3 216.4 all-gather.8
  530.2 216.3 all-gather.10
  769.6 58.9 reduce-scatter.1
